TPU v7x, 32 devices: a whole 2x2x4 slice. The times are simulated.
32 devices in a mesh: frame: 32 (over z, y, x, core), segment: 1.
Axes of the slice: x: 2, y: 2, z: 4, core: 2. Of those that a mesh axis runs over, the one named last changes fastest.
Arguments:
- state: bfloat16 [1, 1024, 3072], P('segment', 'frame'), may hold values from -6 to 6
- modulation: float32 [1, 32, 7, 3072], P('segment'), may hold values from -3 to 3
- noise_level: int32 [4], replicated, may hold values from 0 to 31
- frame_mask: int32 [4, 4], replicated, may hold values from 0 to 1, as said below
- offset: int32 [1], replicated, may hold values from 1 to 3
Outputs:
- next_state: bfloat16 [1, 1024, 3072], P('segment', 'frame')
Inputs may be any that keep to these rules, and one draw needn't show every extreme that they name: frame_mask[i, i] is 1 and frame_mask[i, j] is 0 for j > i.
All inputs are finite; a program needn't handle non-finite values.
Results may differ from a plain program's by a relative error of at most 0.017.
Values may be sent and summed in bfloat16 or wider, within the bound.
A program may use at most 128 MiB of HBM per device.

v0:
```python
import functools
import math

import jax
import jax.numpy as jnp
from jax import lax
from jax.experimental import pallas as pl
from jax.experimental.pallas import tpu as pltpu
from jax.sharding import PartitionSpec as P

HEAD = 128
FRAME_TOK = 256

epsilon = 1e-06
negative = -1e30


def kernel(
    devices,
    segments,
    heads,
    frames,
    rows,
    level_ref,
    mask_ref,
    offset_ref,
    state_ref,
    mod_ref,
    out_ref,
    local,
    gathered,
    scale_out,
    scales,
    mods,
    normed,
    keys,
    values,
    outgoing,
    local_sem,
    mod_sem,
    state_send,
    state_recv,
    scale_send,
    scale_recv,
    out_send,
    out_recv,
):
    me = lax.axis_index("frame")
    segment = lax.axis_index("segment")
    span = FRAME_TOK // rows
    width = heads * HEAD
    def owner_of(head):
        return lax.div(head * devices, heads)

    my_head = lax.min(lax.div(me * heads + devices - 1, devices), heads - 1)
    owner = owner_of(my_head) == me
    group = max(heads * span // devices, 1)
    group = group if heads % group == 0 else 1
    my_columns = pl.multiple_of(my_head * HEAD, HEAD)
    my_frame = lax.div(me, span)
    my_row = pl.multiple_of(lax.rem(me, span) * rows, rows)

    nxt = lax.rem(segment + 1, segments)
    barrier = pltpu.get_barrier_semaphore()

    def greet(peer, peer_segment):
        pl.semaphore_signal(
            barrier,
            inc=1,
            device_id={"frame": peer, "segment": peer_segment},
            device_id_type=pl.DeviceIdType.MESH,
        )

    def greet_reader(index, carry):
        greet(lax.rem(me + index, devices), segment)
        return carry

    def greet_writer(head, carry):
        greet(owner_of(head), lax.rem(segment + segments - 1, segments))
        return carry

    fetch = pltpu.make_async_copy(state_ref.at[0], local, local_sem)
    fetch.start()

    @pl.when(owner)
    def _():
        lax.fori_loop(1, devices, greet_reader, 0)
        pltpu.make_async_copy(
            mod_ref.at[0, :, :, pl.ds(my_columns, HEAD)], mods, mod_sem
        ).start()

    if segments > 1:
        lax.fori_loop(0, heads, greet_writer, 0)

    fetch.wait()
    greetings = heads - jnp.where(owner, 1, 0)
    if segments > 1:
        greetings += jnp.where(owner, devices, 0)
    pl.semaphore_wait(barrier, greetings)

    def state_copy(head):
        columns = pl.ds(pl.multiple_of(head * HEAD, HEAD), HEAD)
        return pltpu.make_async_remote_copy(
            src_ref=local.at[:, columns],
            dst_ref=gathered.at[my_frame, pl.ds(my_row, rows), :],
            send_sem=state_send.at[head],
            recv_sem=state_recv.at[my_frame],
            device_id={"frame": owner_of(head)},
            device_id_type=pl.DeviceIdType.MESH,
        )

    def scale_copy(head):
        return pltpu.make_async_remote_copy(
            src_ref=scale_out,
            dst_ref=scales.at[me],
            send_sem=scale_send.at[head],
            recv_sem=scale_recv.at[my_frame],
            device_id={"frame": owner_of(head)},
            device_id_type=pl.DeviceIdType.MESH,
        )

    def for_heads(act):
        def step(index, carry):
            turned = index - lax.rem(index, group) + lax.rem(index + me, group)
            head = lax.rem(lax.div(me * heads, devices) + index, heads)

            @pl.when(owner_of(head) != me)
            def _():
                act(head)

            return carry

        lax.fori_loop(0, heads, step, 0)

    def end_rows(head):
        state_copy(head).wait_send()
        scale_copy(head).wait_send()

    for_heads(lambda head: state_copy(head).start())

    @pl.when(owner)
    def _():
        pltpu.make_async_copy(
            local.at[:, pl.ds(my_columns, HEAD)],
            gathered.at[my_frame, pl.ds(my_row, rows), :],
            state_recv.at[my_frame],
        ).start()

    widened = local[...].astype(jnp.float32)
    square_mean = jnp.sum(widened * widened, axis=-1, keepdims=True) * (1.0 / width)
    factor = lax.rsqrt(square_mean + epsilon)
    diagonal = lax.broadcasted_iota(jnp.int32, (rows, HEAD), 0) == lax.broadcasted_iota(
        jnp.int32, (rows, HEAD), 1
    )
    scale_out[...] = jnp.sum(
        jnp.where(diagonal, factor, 0.0), axis=0, keepdims=True
    )

    for_heads(lambda head: scale_copy(head).start())

    @pl.when(owner)
    def _():
        pltpu.make_async_copy(scale_out, scales.at[me], scale_recv.at[my_frame]).start()

    def mods_of(frame):
        level = level_ref[frame]
        return lambda kind: mods[kind, pl.ds(level, 1), :]

    def out_copy(place, part):
        target = place * span + part
        return target, pltpu.make_async_remote_copy(
            src_ref=outgoing.at[place, pl.ds(pl.multiple_of(part * rows, rows), rows), :],
            dst_ref=out_ref.at[my_head],
            send_sem=out_send.at[target],
            recv_sem=out_recv,
            device_id={"frame": target, "segment": nxt},
            device_id_type=pl.DeviceIdType.MESH,
        )

    def send_place(place, begin):
        def step(part, carry):
            target, copy = out_copy(place, part)
            remote = jnp.logical_or(target != me, nxt != segment)

            @pl.when(remote)
            def _():
                if begin:
                    copy.start()
                else:
                    copy.wait_send()

            if begin:
                @pl.when(jnp.logical_not(remote))
                def _():
                    pltpu.make_async_copy(
                        outgoing.at[place, pl.ds(pl.multiple_of(part * rows, rows), rows), :],
                        out_ref.at[my_head],
                        out_recv,
                    ).start()

            return carry

        lax.fori_loop(0, span, step, 0)

    @pl.when(owner)
    def _():
        values[:, HEAD:] = jnp.ones((frames * FRAME_TOK, HEAD), jnp.bfloat16)
        pltpu.make_async_copy(
            mod_ref.at[0, :, :, pl.ds(my_columns, HEAD)], mods, mod_sem
        ).wait()
        for frame in range(frames):
            pltpu.make_async_copy(
                gathered.at[frame], gathered.at[frame], state_recv.at[frame]
            ).wait()
            arrived = scales.at[pl.ds(frame * span, span)]
            pltpu.make_async_copy(arrived, arrived, scale_recv.at[frame]).wait()
            row_mods = mods_of(frame)
            for part in range(span):
                column = jnp.sum(
                    jnp.where(diagonal, scales[frame * span + part], 0.0),
                    axis=1,
                    keepdims=True,
                )
                inner = slice(part * rows, (part + 1) * rows)
                outer = slice(frame * FRAME_TOK + part * rows, frame * FRAME_TOK + (part + 1) * rows)
                scaled = (
                    gathered[frame, inner, :].astype(jnp.float32) * column
                ).astype(jnp.bfloat16)
                normed[frame, inner, :] = scaled
                wide = scaled.astype(jnp.float32)
                keys[outer, :] = (
                    wide * (1.0 + row_mods(2)) + row_mods(3)
                ).astype(jnp.bfloat16)
                values[outer, :HEAD] = (
                    wide * (1.0 + row_mods(4)) + row_mods(5)
                ).astype(jnp.bfloat16)

        shift = jnp.where(segment == segments - 1, offset_ref[0], 0)
        for turn in range(frames):
            place = jnp.where(2 * me >= devices, turn, (frames - turn) % frames)
            frame = lax.rem(place + shift, frames)
            row_mods = mods_of(frame)
            queries = (
                normed[frame].astype(jnp.float32) * (1.0 + row_mods(0)) + row_mods(1)
            ).astype(jnp.bfloat16)
            bias = jnp.concatenate(
                [
                    jnp.full(
                        (1, FRAME_TOK),
                        jnp.where(mask_ref[frame, other] == 1, 0.0, negative),
                        jnp.float32,
                    )
                    for other in range(frames)
                ],
                axis=1,
            )
            scores = lax.dot_general(
                queries,
                keys[...],
                (((1,), (1,)), ((), ())),
                preferred_element_type=jnp.float32,
            )
            scores = scores * (1.0 / math.sqrt(HEAD)) + bias
            weights = jnp.exp(scores - jnp.max(scores, axis=-1, keepdims=True)).astype(
                jnp.bfloat16
            )
            summed = jnp.dot(weights, values[...], preferred_element_type=jnp.float32)
            attention = (summed[:, :HEAD] / summed[:, HEAD:]).astype(jnp.bfloat16)
            outgoing[place] = (
                gathered[frame].astype(jnp.float32)
                + row_mods(6) * attention.astype(jnp.float32)
            ).astype(jnp.bfloat16)
            send_place(place, True)

    for_heads(end_rows)

    @pl.when(owner)
    def _():
        for place in range(frames):
            send_place(place, False)

    pltpu.make_async_copy(out_ref, out_ref, out_recv).wait()


def body(state, modulation, noise_level, frame_mask, offset):
    _, rows, width = state.shape
    _, levels, kinds, _ = modulation.shape
    devices = lax.axis_size("frame")
    segments = lax.axis_size("segment")
    heads = width // HEAD
    frames = devices * rows // FRAME_TOK
    tokens = devices * rows
    smem = pl.BlockSpec(memory_space=pltpu.SMEM)
    hbm = pl.BlockSpec(memory_space=pl.ANY)
    tiles = pl.pallas_call(
        functools.partial(kernel, devices, segments, heads, frames, rows),
        out_shape=pltpu.VMEM((heads, rows, HEAD), jnp.bfloat16),
        in_specs=[smem, smem, smem, hbm, hbm],
        out_specs=pl.BlockSpec(memory_space=pltpu.VMEM),
        scratch_shapes=[
            pltpu.VMEM((rows, width), jnp.bfloat16),
            pltpu.VMEM((frames, FRAME_TOK, HEAD), jnp.bfloat16),
            pltpu.VMEM((1, HEAD), jnp.float32),
            pltpu.VMEM((devices, 1, HEAD), jnp.float32),
            pltpu.VMEM((kinds, levels, HEAD), jnp.float32),
            pltpu.VMEM((frames, FRAME_TOK, HEAD), jnp.bfloat16),
            pltpu.VMEM((tokens, HEAD), jnp.bfloat16),
            pltpu.VMEM((tokens, 2 * HEAD), jnp.bfloat16),
            pltpu.VMEM((frames, FRAME_TOK, HEAD), jnp.bfloat16),
            pltpu.SemaphoreType.DMA,
            pltpu.SemaphoreType.DMA,
            pltpu.SemaphoreType.DMA((heads,)),
            pltpu.SemaphoreType.DMA((frames,)),
            pltpu.SemaphoreType.DMA((heads,)),
            pltpu.SemaphoreType.DMA((frames,)),
            pltpu.SemaphoreType.DMA((devices,)),
            pltpu.SemaphoreType.DMA,
        ],
        compiler_params=pltpu.CompilerParams(has_side_effects=True, collective_id=0),
        name="denoise",
    )(noise_level, frame_mask, offset, state, jnp.swapaxes(modulation, 1, 2))
    return jnp.swapaxes(tiles, 0, 1).reshape(state.shape)


def solution(mesh):
    return jax.shard_map(
        body,
        mesh=mesh,
        in_specs=(P("segment", "frame", None), P("segment", None, None, None), P(), P(), P()),
        out_specs=P("segment", "frame", None),
        check_vma=False,
    )
```

profile of v0, /device:TPU:0, one launch (start us, length us, event | category | flops | bytes accessed | tf_op | source)
XLA Modules:
  0.0 23.3 jit_solution(3283982210998889472)
XLA Ops:
  0.7 21.8 %denoise.1 = bf16[24,32,128]{2,1,0:T(8,128)(2,1)S(1)} custom-call(s32[4]{0:T(128)} %level_ref.1, s32[4,4]{1,0:T(4,128)} %mask_ref.1, s32[1]{0:T(128)S(6)} %copy.7.offset_ref, bf16[1,32,3072]{2,1,0:T(8,128)(2,1)} %state_ref.1, f32[1,7,32,3072]{3,2,1,0:T(8,128)} %bitcast.3), custom_call_target="tpu_custom_call" | custom-call | tf_op jit(solution)/shard_map/denoise/pallas_call | solution.py:295
  22.4 0.1 copy.6
  22.5 0.8 %reshape.3 = bf16[1,32,3072]{2,1,0:T(8,128)(2,1)} reshape(bf16[32,24,128]{2,1,0:T(8,128)(2,1)S(1)} %copy.6) | data formatting | bytes 393216 | tf_op jit(solution)/shard_map/reshape | solution.py:322
where the time goes:
time: 23.6 us; the launch traced here: 23.3 us
  Pallas kernels  21.8 us (92%)
  local copies, waits for them, and re-layouts  0.84 us (4%)
  between operations  0.67 us (3%)
    pallas_call x1, Pallas kernels, body(): pl.pallas_call(functools.partial(kernel, devices, segments, heads, frames...  21.8 us
    reshape x1, local copies, waits for them, and re-layouts, body(): return jnp.swapaxes(tiles, 0, 1).reshape(state.shape)  0.76 us

commit v1 on v0

v1 whole, which is shorter than its diff:
```python
import functools
import math

import jax
import jax.numpy as jnp
from jax import lax
from jax.experimental import pallas as pl
from jax.experimental.pallas import tpu as pltpu
from jax.sharding import PartitionSpec as P

HEAD = 128
FRAME_TOK = 256

epsilon = 1e-06
negative = -1e30
score_scale = math.log2(math.e) / math.sqrt(HEAD)


def kernel(
    devices,
    segments,
    heads,
    frames,
    rows,
    level_hbm,
    mask_hbm,
    offset_hbm,
    state_ref,
    mod_ref,
    out_ref,
    level_ref,
    mask_ref,
    offset_ref,
    local,
    gathered,
    scale_out,
    scales,
    mods,
    keys,
    values,
    done,
    outgoing,
    scalar_sem,
    local_sem,
    mod_sem,
    state_send,
    state_recv,
    scale_send,
    scale_recv,
    out_send,
    out_recv,
):
    me = lax.axis_index("frame")
    segment = lax.axis_index("segment")
    span = FRAME_TOK // rows
    width = heads * HEAD
    def owner_of(head):
        return head

    my_frame = lax.div(me, span)
    my_part = lax.rem(me, span)
    my_head = lax.min(me, heads - 1)
    owner = me < heads
    my_columns = pl.multiple_of(my_head * HEAD, HEAD)
    my_row = pl.multiple_of(my_part * rows, rows)

    nxt = lax.rem(segment + 1, segments)
    barrier = pltpu.get_barrier_semaphore()

    def greet(peer, peer_segment):
        pl.semaphore_signal(
            barrier,
            inc=1,
            device_id={"frame": peer, "segment": peer_segment},
            device_id_type=pl.DeviceIdType.MESH,
        )

    def greet_reader(index, carry):
        greet(index + jnp.where(index >= me, 1, 0), segment)
        return carry

    def greet_writer(head, carry):
        greet(owner_of(head), lax.rem(segment + segments - 1, segments))
        return carry

    fetch = pltpu.make_async_copy(state_ref.at[0], local, local_sem)
    fetch.start()

    @pl.when(owner)
    def _():
        lax.fori_loop(0, devices - 1, greet_reader, 0)

    if segments > 1:
        lax.fori_loop(0, heads, greet_writer, 0)

    scalar_copies = [
        pltpu.make_async_copy(source, place, scalar_sem.at[index])
        for index, (source, place) in enumerate(
            ((level_hbm, level_ref), (mask_hbm, mask_ref), (offset_hbm, offset_ref))
        )
    ]
    mod_copy = pltpu.make_async_copy(
        mod_ref.at[0, :, :, pl.ds(my_columns, HEAD)], mods, mod_sem
    )

    @pl.when(owner)
    def _():
        mod_copy.start()
        for copy in scalar_copies:
            copy.start()

    fetch.wait()
    widened = local[...].astype(jnp.float32)
    square_mean = jnp.sum(widened * widened, axis=-1, keepdims=True) * (1.0 / width)
    factor = lax.rsqrt(square_mean + epsilon)
    diagonal = lax.broadcasted_iota(jnp.int32, (rows, HEAD), 0) == lax.broadcasted_iota(
        jnp.int32, (rows, HEAD), 1
    )
    scale_out[...] = jnp.sum(
        jnp.where(diagonal, factor, 0.0), axis=0, keepdims=True
    )

    greetings = heads - jnp.where(owner, 1, 0)
    if segments > 1:
        greetings += jnp.where(owner, devices, 0)
    pl.semaphore_wait(barrier, greetings)

    def state_copy(head):
        columns = pl.ds(pl.multiple_of(head * HEAD, HEAD), HEAD)
        return pltpu.make_async_remote_copy(
            src_ref=local.at[:, columns],
            dst_ref=gathered.at[my_frame, pl.ds(my_row, rows), :],
            send_sem=state_send.at[head],
            recv_sem=state_recv.at[my_frame],
            device_id={"frame": owner_of(head)},
            device_id_type=pl.DeviceIdType.MESH,
        )

    def scale_copy(head):
        return pltpu.make_async_remote_copy(
            src_ref=scale_out,
            dst_ref=scales.at[me],
            send_sem=scale_send.at[head],
            recv_sem=scale_recv.at[my_frame],
            device_id={"frame": owner_of(head)},
            device_id_type=pl.DeviceIdType.MESH,
        )

    def for_heads(act):
        part = heads // 2
        begin = lax.rem(lax.div(me, 2) + 0, part)

        for turn in range(2):
            def step(index, carry):
                place = begin + index
                head = 2 * jnp.where(place >= part, place - part, place) + turn

                @pl.when(owner_of(head) != me)
                def _():
                    act(head)

                return carry

            lax.fori_loop(0, part, step, 0)

    def send_rows(head):
        state_copy(head).start()
        scale_copy(head).start()

    def end_rows(head):
        state_copy(head).wait_send()
        scale_copy(head).wait_send()

    for_heads(send_rows)

    @pl.when(owner)
    def _():
        pltpu.make_async_copy(
            local.at[:, pl.ds(my_columns, HEAD)],
            gathered.at[my_frame, pl.ds(my_row, rows), :],
            state_recv.at[my_frame],
        ).start()
        pltpu.make_async_copy(scale_out, scales.at[me], scale_recv.at[my_frame]).start()

    def out_copy(place, part):
        target = place * span + part
        return target, pltpu.make_async_remote_copy(
            src_ref=outgoing.at[place, pl.ds(pl.multiple_of(part * rows, rows), rows), :],
            dst_ref=out_ref.at[0, :, pl.ds(my_columns, HEAD)],
            send_sem=out_send.at[target],
            recv_sem=out_recv,
            device_id={"frame": target, "segment": nxt},
            device_id_type=pl.DeviceIdType.MESH,
        )

    def send_part(place, part, begin):
        target, copy = out_copy(place, part)
        remote = jnp.logical_or(target != me, nxt != segment)

        @pl.when(remote)
        def _():
            if begin:
                copy.start()
            else:
                copy.wait_send()

        if begin:
            @pl.when(jnp.logical_not(remote))
            def _():
                pltpu.make_async_copy(
                    outgoing.at[place, pl.ds(pl.multiple_of(part * rows, rows), rows), :],
                    out_ref.at[0, :, pl.ds(my_columns, HEAD)],
                    out_recv,
                ).start()

    def send_place(place, begin):
        def step(part, carry):
            send_part(place, part, begin)
            return carry

        lax.fori_loop(0, span, step, 0)

    def mod_row(frame, kind):
        return mods[kind, pl.ds(level_ref[frame], 1), :]

    def project(frame):
        query_scale = (1.0 + mod_row(frame, 0)) * score_scale
        query_shift = mod_row(frame, 1) * score_scale
        key_scale, key_shift = 1.0 + mod_row(frame, 2), mod_row(frame, 3)
        value_scale, value_shift = 1.0 + mod_row(frame, 4), mod_row(frame, 5)
        queries = []
        for part in range(span):
            column = jnp.sum(
                jnp.where(diagonal, scales[frame * span + part], 0.0), axis=1, keepdims=True
            )
            inner = slice(part * rows, (part + 1) * rows)
            outer = slice(frame * FRAME_TOK + part * rows, frame * FRAME_TOK + (part + 1) * rows)
            wide = (
                (gathered[frame, inner, :].astype(jnp.float32) * column)
                .astype(jnp.bfloat16)
                .astype(jnp.float32)
            )
            keys[outer, :] = (wide * key_scale + key_shift).astype(jnp.bfloat16)
            values[outer, :] = (wide * value_scale + value_shift).astype(jnp.bfloat16)
            queries.append((wide * query_scale + query_shift).astype(jnp.bfloat16))
        return jnp.concatenate(queries, axis=0)

    def attend(frame, queries):
        def tokens_of(other):
            return slice(other * FRAME_TOK, (other + 1) * FRAME_TOK)

        scores = [
            lax.dot_general(
                queries,
                keys[tokens_of(other), :],
                (((1,), (1,)), ((), ())),
                preferred_element_type=jnp.float32,
            )
            for other in range(frame + 1)
        ]
        top = jnp.max(scores[frame], axis=-1, keepdims=True)
        for other in range(frame):
            peak = jnp.max(scores[other], axis=-1, keepdims=True)
            top = jnp.maximum(top, jnp.where(mask_ref[frame, other] == 1, peak, negative))
        summed, total = 0.0, 0.0
        for other in range(frame + 1):
            floor = top
            if other < frame:
                floor = top + jnp.where(mask_ref[frame, other] == 1, 0.0, -negative)
            weights = jnp.exp2(scores[other] - floor).astype(jnp.bfloat16)
            total += jnp.sum(weights.astype(jnp.float32), axis=-1, keepdims=True)
            summed += jnp.dot(
                weights, values[tokens_of(other), :], preferred_element_type=jnp.float32
            )
        attention = (summed / total).astype(jnp.bfloat16)
        done[frame] = (
            gathered[frame].astype(jnp.float32)
            + mod_row(frame, 6) * attention.astype(jnp.float32)
        ).astype(jnp.bfloat16)

    @pl.when(owner)
    def _():
        mod_copy.wait()
        for copy in scalar_copies:
            copy.wait()
        for batch in [[f] for f in range(frames)]:
            for frame in batch:
                pltpu.make_async_copy(
                    gathered.at[frame], gathered.at[frame], state_recv.at[frame]
                ).wait()
                arrived = scales.at[pl.ds(frame * span, span)]
                pltpu.make_async_copy(arrived, arrived, scale_recv.at[frame]).wait()
            held = [project(frame) for frame in batch]
            for frame, queries in zip(batch, held):
                attend(frame, queries)

        shift = jnp.where(segment == segments - 1, offset_ref[0], 0)
        for place in range(frames):
            outgoing[place] = done[lax.rem(place + shift, frames)]

        def send_all(index, carry):
            part = lax.rem(index + 0, span)
            for place in (3, 2, 1, 0):
                send_part(place, part, True)
            return carry

        lax.fori_loop(0, span, send_all, 0)

    for_heads(end_rows)

    @pl.when(owner)
    def _():
        for place in range(frames):
            send_place(place, False)

    pltpu.make_async_copy(out_ref, out_ref, out_recv).wait()


def body(state, modulation, noise_level, frame_mask, offset):
    _, rows, width = state.shape
    _, levels, kinds, _ = modulation.shape
    devices = lax.axis_size("frame")
    segments = lax.axis_size("segment")
    heads = width // HEAD
    frames = devices * rows // FRAME_TOK
    tokens = devices * rows
    hbm = pl.BlockSpec(memory_space=pl.ANY)
    return pl.pallas_call(
        functools.partial(kernel, devices, segments, heads, frames, rows),
        out_shape=pltpu.VMEM(state.shape, jnp.bfloat16),
        in_specs=[hbm] * 5,
        out_specs=pl.BlockSpec(memory_space=pltpu.VMEM),
        scratch_shapes=[
            pltpu.SMEM(noise_level.shape, jnp.int32),
            pltpu.SMEM(frame_mask.shape, jnp.int32),
            pltpu.SMEM(offset.shape, jnp.int32),
            pltpu.VMEM((rows, width), jnp.bfloat16),
            pltpu.VMEM((frames, FRAME_TOK, HEAD), jnp.bfloat16),
            pltpu.VMEM((1, HEAD), jnp.float32),
            pltpu.VMEM((devices, 1, HEAD), jnp.float32),
            pltpu.VMEM((kinds, levels, HEAD), jnp.float32),
            pltpu.VMEM((tokens, HEAD), jnp.bfloat16),
            pltpu.VMEM((tokens, HEAD), jnp.bfloat16),
            pltpu.VMEM((frames, FRAME_TOK, HEAD), jnp.bfloat16),
            pltpu.VMEM((frames, FRAME_TOK, HEAD), jnp.bfloat16),
            pltpu.SemaphoreType.DMA((3,)),
            pltpu.SemaphoreType.DMA,
            pltpu.SemaphoreType.DMA,
            pltpu.SemaphoreType.DMA((heads,)),
            pltpu.SemaphoreType.DMA((frames,)),
            pltpu.SemaphoreType.DMA((heads,)),
            pltpu.SemaphoreType.DMA((frames,)),
            pltpu.SemaphoreType.DMA((devices,)),
            pltpu.SemaphoreType.DMA,
        ],
        compiler_params=pltpu.CompilerParams(has_side_effects=True, collective_id=0),
        name="denoise",
    )(noise_level, frame_mask, offset, state, jnp.swapaxes(modulation, 1, 2))


def solution(mesh):
    return jax.shard_map(
        body,
        mesh=mesh,
        in_specs=(P("segment", "frame", None), P("segment", None, None, None), P(), P(), P()),
        out_specs=P("segment", "frame", None),
        check_vma=False,
    )
```

time: 23.6 us -> 21.2 us (0.90)
  Pallas kernels: 21.8 us -> 19.6 us
    pallas_call x1, Pallas kernels: 21.8 us -> 19.6 us  [body(): pl.pallas_call(functools.partial(kernel, devices, segments, heads, frames...]
    reshape x1 -> x0, local copies, waits for them, and re-layouts: 0.76 us -> none  [body(): return jnp.swapaxes(tiles, 0, 1).reshape(state.shape)]
    unnamed x0 -> x1, local copies, waits for them, and re-layouts: none -> 0.68 us
where the time goes in v1:
time: 21.2 us; the launch traced here: 20.9 us
  Pallas kernels  19.6 us (92%)
  local copies, waits for them, and re-layouts  0.68 us (3%)
  between operations  0.66 us (3%)
    pallas_call x1, Pallas kernels, body(): pl.pallas_call(functools.partial(kernel, devices, segments, heads, frames...  19.6 us
    unnamed x1, local copies, waits for them, and re-layouts  0.68 us

profile of v1, /device:TPU:0, one launch (start us, length us, event | category | flops | bytes accessed | tf_op | source)
XLA Modules:
  0.0 20.9 jit_solution(8435058923656933000)
XLA Ops:
  0.7 19.6 %denoise.1 = bf16[1,32,3072]{2,1,0:T(8,128)(2,1)S(1)} custom-call(s32[4]{0:T(128)} %level_hbm.1, s32[4,4]{1,0:T(4,128)} %mask_hbm.1, s32[1]{0:T(128)S(6)} %copy.8.offset_hbm, bf16[1,32,3072]{2,1,0:T(8,128)(2,1)} %state_ref.1, f32[1,7,32,3072]{3,2,1,0:T(8,128)} %bitcast.1), custom_call_target="tpu_custom_call" | custom-call | tf_op jit(solution)/shard_map/denoise/pallas_call | solution.py:328
  20.2 0.7 %copy.7 = bf16[1,32,3072]{2,1,0:T(8,128)(2,1)} copy(bf16[1,32,3072]{2,1,0:T(8,128)(2,1)S(1)} %denoise.1) | data formatting | bytes 393216

commit v2 on v1

--- a/solution.py
+++ b/solution.py
@@ -14,6 +14,14 @@
 epsilon = 1e-06
 negative = -1e30
 score_scale = math.log2(math.e) / math.sqrt(HEAD)
+
+
+def owner_rounds(heads, span):
+    if heads % span or span % 2:
+        return [(0, 1, heads)]
+    groups = heads // span
+    evens = [(group * span, 2, span // 2) for group in [*range(1, groups), 0]]
+    return evens + [(first + 1, 2, count) for first, _, count in reversed(evens)]
 
 
 def kernel(
@@ -54,18 +62,30 @@
     segment = lax.axis_index("segment")
     span = FRAME_TOK // rows
     width = heads * HEAD
-    def owner_of(head):
-        return head
-
+    plan = owner_rounds(heads, span)
     my_frame = lax.div(me, span)
     my_part = lax.rem(me, span)
-    my_head = lax.min(me, heads - 1)
-    owner = me < heads
-    my_columns = pl.multiple_of(my_head * HEAD, HEAD)
     my_row = pl.multiple_of(my_part * rows, rows)
+
+    owner, my_head, base = me < 0, 0, 0
+    rounds = []
+    for first, stride, count in plan:
+        rounds.append((base, first, stride, count))
+        place = me - first
+        inside = jnp.logical_and(place >= 0, place < stride * count)
+        if stride > 1:
+            inside = jnp.logical_and(inside, lax.rem(place + stride * devices, stride) == 0)
+        owner = jnp.logical_or(owner, inside)
+        my_head = jnp.where(inside, base + lax.div(place, stride), my_head)
+        if base == 0:
+            early = inside
+        base += count
 
     nxt = lax.rem(segment + 1, segments)
     barrier = pltpu.get_barrier_semaphore()
+
+    def columns_of(head):
+        return pl.ds(pl.multiple_of(head * HEAD, HEAD), HEAD)
 
     def greet(peer, peer_segment):
         pl.semaphore_signal(
@@ -79,19 +99,29 @@
         greet(index + jnp.where(index >= me, 1, 0), segment)
         return carry
 
-    def greet_writer(head, carry):
-        greet(owner_of(head), lax.rem(segment + segments - 1, segments))
-        return carry
-
-    fetch = pltpu.make_async_copy(state_ref.at[0], local, local_sem)
-    fetch.start()
+    fetches = [
+        pltpu.make_async_copy(
+            state_ref.at[0, :, pl.ds(piece * (width // 1), width // 1)],
+            local.at[:, pl.ds(piece * (width // 1), width // 1)],
+            local_sem.at[piece],
+        )
+        for piece in range(1)
+    ]
+    for fetch in fetches:
+        fetch.start()
 
     @pl.when(owner)
     def _():
         lax.fori_loop(0, devices - 1, greet_reader, 0)
 
     if segments > 1:
-        lax.fori_loop(0, heads, greet_writer, 0)
+        for _, first, stride, count in rounds:
+
+            def greet_writer(index, carry):
+                greet(first + stride * index, lax.rem(segment + segments - 1, segments))
+                return carry
+
+            lax.fori_loop(0, count, greet_writer, 0)
 
     scalar_copies = [
         pltpu.make_async_copy(source, place, scalar_sem.at[index])
@@ -100,7 +130,7 @@
         )
     ]
     mod_copy = pltpu.make_async_copy(
-        mod_ref.at[0, :, :, pl.ds(my_columns, HEAD)], mods, mod_sem
+        mod_ref.at[0, :, :, columns_of(my_head)], mods, mod_sem
     )
 
     @pl.when(owner)
@@ -109,7 +139,8 @@
         for copy in scalar_copies:
             copy.start()
 
-    fetch.wait()
+    for fetch in fetches:
+        fetch.wait()
     widened = local[...].astype(jnp.float32)
     square_mean = jnp.sum(widened * widened, axis=-1, keepdims=True) * (1.0 / width)
     factor = lax.rsqrt(square_mean + epsilon)
@@ -125,76 +156,67 @@
         greetings += jnp.where(owner, devices, 0)
     pl.semaphore_wait(barrier, greetings)
 
-    def state_copy(head):
-        columns = pl.ds(pl.multiple_of(head * HEAD, HEAD), HEAD)
-        return pltpu.make_async_remote_copy(
-            src_ref=local.at[:, columns],
-            dst_ref=gathered.at[my_frame, pl.ds(my_row, rows), :],
-            send_sem=state_send.at[head],
-            recv_sem=state_recv.at[my_frame],
-            device_id={"frame": owner_of(head)},
-            device_id_type=pl.DeviceIdType.MESH,
-        )
-
-    def scale_copy(head):
-        return pltpu.make_async_remote_copy(
-            src_ref=scale_out,
-            dst_ref=scales.at[me],
-            send_sem=scale_send.at[head],
-            recv_sem=scale_recv.at[my_frame],
-            device_id={"frame": owner_of(head)},
-            device_id_type=pl.DeviceIdType.MESH,
+    def copies_to(head, peer):
+        return (
+            pltpu.make_async_remote_copy(
+                src_ref=local.at[:, columns_of(head)],
+                dst_ref=gathered.at[my_frame, pl.ds(my_row, rows), :],
+                send_sem=state_send.at[head],
+                recv_sem=state_recv.at[my_frame],
+                device_id={"frame": peer},
+                device_id_type=pl.DeviceIdType.MESH,
+            ),
+            pltpu.make_async_remote_copy(
+                src_ref=scale_out,
+                dst_ref=scales.at[me],
+                send_sem=scale_send.at[head],
+                recv_sem=scale_recv.at[my_frame],
+                device_id={"frame": peer},
+                device_id_type=pl.DeviceIdType.MESH,
+            ),
         )
 
     def for_heads(act):
-        part = heads // 2
-        begin = lax.rem(lax.div(me, 2) + 0, part)
-
-        for turn in range(2):
-            def step(index, carry):
-                place = begin + index
-                head = 2 * jnp.where(place >= part, place - part, place) + turn
-
-                @pl.when(owner_of(head) != me)
+        for base, first, stride, count in rounds:
+            turn = lax.rem(lax.div(me, 2) + 1, count)
+
+            def each(index, carry):
+                index += turn
+                index = jnp.where(index >= count, index - count, index)
+                peer = first + stride * index
+
+                @pl.when(peer != me)
                 def _():
-                    act(head)
+                    for copy in copies_to(base + index, peer):
+                        act(copy)
 
                 return carry
 
-            lax.fori_loop(0, part, step, 0)
-
-    def send_rows(head):
-        state_copy(head).start()
-        scale_copy(head).start()
-
-    def end_rows(head):
-        state_copy(head).wait_send()
-        scale_copy(head).wait_send()
-
-    for_heads(send_rows)
+            lax.fori_loop(0, count, each, 0)
+
+    for_heads(lambda copy: copy.start())
 
     @pl.when(owner)
     def _():
         pltpu.make_async_copy(
-            local.at[:, pl.ds(my_columns, HEAD)],
+            local.at[:, columns_of(my_head)],
             gathered.at[my_frame, pl.ds(my_row, rows), :],
             state_recv.at[my_frame],
         ).start()
         pltpu.make_async_copy(scale_out, scales.at[me], scale_recv.at[my_frame]).start()
 
-    def out_copy(place, part):
+    def send_part(place, part, begin):
         target = place * span + part
-        return target, pltpu.make_async_remote_copy(
-            src_ref=outgoing.at[place, pl.ds(pl.multiple_of(part * rows, rows), rows), :],
-            dst_ref=out_ref.at[0, :, pl.ds(my_columns, HEAD)],
+        source = outgoing.at[place, pl.ds(pl.multiple_of(part * rows, rows), rows), :]
+        goal = out_ref.at[0, :, columns_of(my_head)]
+        copy = pltpu.make_async_remote_copy(
+            src_ref=source,
+            dst_ref=goal,
             send_sem=out_send.at[target],
             recv_sem=out_recv,
             device_id={"frame": target, "segment": nxt},
             device_id_type=pl.DeviceIdType.MESH,
         )
-
-    def send_part(place, part, begin):
-        target, copy = out_copy(place, part)
         remote = jnp.logical_or(target != me, nxt != segment)
 
         @pl.when(remote)
@@ -207,18 +229,20 @@
         if begin:
             @pl.when(jnp.logical_not(remote))
             def _():
-                pltpu.make_async_copy(
-                    outgoing.at[place, pl.ds(pl.multiple_of(part * rows, rows), rows), :],
-                    out_ref.at[0, :, pl.ds(my_columns, HEAD)],
-                    out_recv,
-                ).start()
-
-    def send_place(place, begin):
-        def step(part, carry):
-            send_part(place, part, begin)
+                pltpu.make_async_copy(source, goal, out_recv).start()
+
+    def send_all(begin):
+        def each(index, carry):
+            part = lax.rem(index + 0, span)
+            for turn in range(frames):
+                place = jnp.where(2 * me >= devices, turn, frames - 1 - turn)
+                send_part(place, part, begin)
             return carry
 
-        lax.fori_loop(0, span, step, 0)
+        lax.fori_loop(0, span, each, 0)
+
+    def tokens_of(frame):
+        return slice(frame * FRAME_TOK, (frame + 1) * FRAME_TOK)
 
     def mod_row(frame, kind):
         return mods[kind, pl.ds(level_ref[frame], 1), :]
@@ -246,9 +270,6 @@
         return jnp.concatenate(queries, axis=0)
 
     def attend(frame, queries):
-        def tokens_of(other):
-            return slice(other * FRAME_TOK, (other + 1) * FRAME_TOK)
-
         scores = [
             lax.dot_general(
                 queries,
@@ -278,12 +299,8 @@
             + mod_row(frame, 6) * attention.astype(jnp.float32)
         ).astype(jnp.bfloat16)
 
-    @pl.when(owner)
-    def _():
-        mod_copy.wait()
-        for copy in scalar_copies:
-            copy.wait()
-        for batch in [[f] for f in range(frames)]:
+    def in_order(batches):
+        for batch in batches:
             for frame in batch:
                 pltpu.make_async_copy(
                     gathered.at[frame], gathered.at[frame], state_recv.at[frame]
@@ -294,24 +311,29 @@
             for frame, queries in zip(batch, held):
                 attend(frame, queries)
 
+    @pl.when(owner)
+    def _():
+        mod_copy.wait()
+        for copy in scalar_copies:
+            copy.wait()
+        @pl.when(jnp.logical_or(2 * me >= devices, early))
+        def _():
+            in_order([list(range(frames))])
+
+        @pl.when(jnp.logical_not(jnp.logical_or(2 * me >= devices, early)))
+        def _():
+            in_order([[f] for f in range(frames - 2)] + [[frames - 2, frames - 1]])
+
         shift = jnp.where(segment == segments - 1, offset_ref[0], 0)
         for place in range(frames):
             outgoing[place] = done[lax.rem(place + shift, frames)]
-
-        def send_all(index, carry):
-            part = lax.rem(index + 0, span)
-            for place in (3, 2, 1, 0):
-                send_part(place, part, True)
-            return carry
-
-        lax.fori_loop(0, span, send_all, 0)
-
-    for_heads(end_rows)
-
-    @pl.when(owner)
-    def _():
-        for place in range(frames):
-            send_place(place, False)
+        send_all(True)
+
+    for_heads(lambda copy: copy.wait_send())
+
+    @pl.when(owner)
+    def _():
+        send_all(False)
 
     pltpu.make_async_copy(out_ref, out_ref, out_recv).wait()
 
@@ -344,7 +366,7 @@
             pltpu.VMEM((frames, FRAME_TOK, HEAD), jnp.bfloat16),
             pltpu.VMEM((frames, FRAME_TOK, HEAD), jnp.bfloat16),
             pltpu.SemaphoreType.DMA((3,)),
-            pltpu.SemaphoreType.DMA,
+            pltpu.SemaphoreType.DMA((1,)),
             pltpu.SemaphoreType.DMA,
             pltpu.SemaphoreType.DMA((heads,)),
             pltpu.SemaphoreType.DMA((frames,)),

time: 21.2 us -> 20.5 us (0.967)
  Pallas kernels: 19.6 us -> 19 us
    pallas_call x1, Pallas kernels: 19.6 us -> 19 us  [body(): pl.pallas_call(functools.partial(kernel, devices, segments, heads, frames...]
where the time goes in v2:
time: 20.5 us; the launch traced here: 20.4 us
  Pallas kernels  19 us (93%)
  local copies, waits for them, and re-layouts  0.68 us (3%)
  between operations  0.66 us (3%)
    pallas_call x1, Pallas kernels, body(): pl.pallas_call(functools.partial(kernel, devices, segments, heads, frames...  19 us
    unnamed x1, local copies, waits for them, and re-layouts  0.68 us

profile of v2, /device:TPU:0, one launch (start us, length us, event | category | flops | bytes accessed | tf_op | source)
XLA Modules:
  0.0 20.4 jit_solution(18052472536232576026)
XLA Ops:
  0.7 19.0 %denoise.1 = bf16[1,32,3072]{2,1,0:T(8,128)(2,1)S(1)} custom-call(s32[4]{0:T(128)} %level_hbm.1, s32[4,4]{1,0:T(4,128)} %mask_hbm.1, s32[1]{0:T(128)S(6)} %copy.8.offset_hbm, bf16[1,32,3072]{2,1,0:T(8,128)(2,1)} %state_ref.1, f32[1,7,32,3072]{3,2,1,0:T(8,128)} %bitcast.1), custom_call_target="tpu_custom_call" | custom-call | tf_op jit(solution)/shard_map/denoise/pallas_call | solution.py:350
  19.7 0.7 %copy.7 = bf16[1,32,3072]{2,1,0:T(8,128)(2,1)} copy(bf16[1,32,3072]{2,1,0:T(8,128)(2,1)S(1)} %denoise.1) | data formatting | bytes 393216

commit v3 on v2

--- a/solution.py
+++ b/solution.py
@@ -57,12 +57,15 @@
     scale_recv,
     out_send,
     out_recv,
+    late_sem,
 ):
     me = lax.axis_index("frame")
     segment = lax.axis_index("segment")
     span = FRAME_TOK // rows
     width = heads * HEAD
     plan = owner_rounds(heads, span)
+    shared = heads % span == 0 and heads // span + 1 == frames
+    last = devices - span
     my_frame = lax.div(me, span)
     my_part = lax.rem(me, span)
     my_row = pl.multiple_of(my_part * rows, rows)
@@ -81,6 +84,21 @@
             early = inside
         base += count
 
+    leader = owner
+    late = me >= last
+    split = frames - 1
+    low, high = 0, frames
+    if shared:
+        for base, first, stride, count in list(rounds):
+            if first < span:
+                rounds.append((base, first + last, stride, count))
+                place = me - last - first
+                inside = jnp.logical_and(place >= 0, lax.rem(place + stride * devices, stride) == 0)
+                my_head = jnp.where(inside, base + lax.div(place, stride), my_head)
+        owner = jnp.logical_or(owner, late)
+        low = jnp.where(late, split, 0)
+        high = jnp.where(me < span, split, frames)
+
     nxt = lax.rem(segment + 1, segments)
     barrier = pltpu.get_barrier_semaphore()
 
@@ -110,9 +128,14 @@
     for fetch in fetches:
         fetch.start()
 
-    @pl.when(owner)
+    @pl.when(leader)
     def _():
         lax.fori_loop(0, devices - 1, greet_reader, 0)
+
+    if shared:
+        @pl.when(late)
+        def _():
+            lax.fori_loop(last, devices - 1, greet_reader, 0)
 
     if segments > 1:
         for _, first, stride, count in rounds:
@@ -151,7 +174,9 @@
         jnp.where(diagonal, factor, 0.0), axis=0, keepdims=True
     )
 
-    greetings = heads - jnp.where(owner, 1, 0)
+    greetings = heads - jnp.where(leader, 1, 0)
+    if shared:
+        greetings += jnp.where(late, span - 1, 0)
     if segments > 1:
         greetings += jnp.where(owner, devices, 0)
     pl.semaphore_wait(barrier, greetings)
@@ -161,7 +186,7 @@
             pltpu.make_async_remote_copy(
                 src_ref=local.at[:, columns_of(head)],
                 dst_ref=gathered.at[my_frame, pl.ds(my_row, rows), :],
-                send_sem=state_send.at[head],
+                send_sem=state_send,
                 recv_sem=state_recv.at[my_frame],
                 device_id={"frame": peer},
                 device_id_type=pl.DeviceIdType.MESH,
@@ -169,15 +194,15 @@
             pltpu.make_async_remote_copy(
                 src_ref=scale_out,
                 dst_ref=scales.at[me],
-                send_sem=scale_send.at[head],
+                send_sem=scale_send,
                 recv_sem=scale_recv.at[my_frame],
                 device_id={"frame": peer},
                 device_id_type=pl.DeviceIdType.MESH,
             ),
         )
 
-    def for_heads(act):
-        for base, first, stride, count in rounds:
+    def for_heads(chosen, act):
+        for base, first, stride, count in chosen:
             turn = lax.rem(lax.div(me, 2) + 1, count)
 
             def each(index, carry):
@@ -194,7 +219,27 @@
 
             lax.fori_loop(0, count, each, 0)
 
-    for_heads(lambda copy: copy.start())
+    for_heads(rounds[: len(plan)], lambda copy: copy.start())
+
+    if shared:
+        def admit(peer, carry):
+            pl.semaphore_signal(
+                late_sem,
+                inc=1,
+                device_id={"frame": peer},
+                device_id_type=pl.DeviceIdType.MESH,
+            )
+            return carry
+
+        @pl.when(late)
+        def _():
+            lax.fori_loop(0, last, admit, 0)
+
+        @pl.when(jnp.logical_not(late))
+        def _():
+            pl.semaphore_wait(late_sem, span)
+
+        for_heads(rounds[len(plan) :], lambda copy: copy.start())
 
     @pl.when(owner)
     def _():
@@ -205,41 +250,49 @@
         ).start()
         pltpu.make_async_copy(scale_out, scales.at[me], scale_recv.at[my_frame]).start()
 
-    def send_part(place, part, begin):
+    def send_part(place, part):
         target = place * span + part
         source = outgoing.at[place, pl.ds(pl.multiple_of(part * rows, rows), rows), :]
         goal = out_ref.at[0, :, columns_of(my_head)]
-        copy = pltpu.make_async_remote_copy(
-            src_ref=source,
-            dst_ref=goal,
-            send_sem=out_send.at[target],
-            recv_sem=out_recv,
-            device_id={"frame": target, "segment": nxt},
-            device_id_type=pl.DeviceIdType.MESH,
-        )
         remote = jnp.logical_or(target != me, nxt != segment)
 
         @pl.when(remote)
         def _():
-            if begin:
-                copy.start()
-            else:
-                copy.wait_send()
-
-        if begin:
-            @pl.when(jnp.logical_not(remote))
-            def _():
-                pltpu.make_async_copy(source, goal, out_recv).start()
-
-    def send_all(begin):
+            pltpu.make_async_remote_copy(
+                src_ref=source,
+                dst_ref=goal,
+                send_sem=out_send,
+                recv_sem=out_recv,
+                device_id={"frame": target, "segment": nxt},
+                device_id_type=pl.DeviceIdType.MESH,
+            ).start()
+
+        @pl.when(jnp.logical_not(remote))
+        def _():
+            pltpu.make_async_copy(source, goal, out_recv).start()
+
+    def send_all():
         def each(index, carry):
-            part = lax.rem(index + 0, span)
-            for turn in range(frames):
-                place = jnp.where(2 * me >= devices, turn, frames - 1 - turn)
-                send_part(place, part, begin)
-            return carry
+            part = index
+
+            def one(turn, carry):
+                place = jnp.where(2 * me >= devices, low + turn, high - 1 - turn)
+                send_part(place, part)
+                return carry
+
+            return lax.fori_loop(0, high - low, one, carry)
 
         lax.fori_loop(0, span, each, 0)
+
+
+    def sent(count, send_sem):
+        pieces = keys.at[pl.ds(0, count * rows), :]
+        pltpu.make_async_copy(pieces, pieces, send_sem).wait()
+
+    def sent_rows(count):
+        sent(count, state_send)
+        factors = scales.at[pl.ds(0, count)]
+        pltpu.make_async_copy(factors, factors, scale_send).wait()
 
     def tokens_of(frame):
         return slice(frame * FRAME_TOK, (frame + 1) * FRAME_TOK)
@@ -327,13 +380,28 @@
         shift = jnp.where(segment == segments - 1, offset_ref[0], 0)
         for place in range(frames):
             outgoing[place] = done[lax.rem(place + shift, frames)]
-        send_all(True)
-
-    for_heads(lambda copy: copy.wait_send())
-
-    @pl.when(owner)
-    def _():
-        send_all(False)
+        send_all()
+
+    kept = 1 if segments == 1 else 0
+    if shared:
+        sent_rows(heads + span - 1)
+        for chosen, count in (
+            (me < span, split),
+            (late, frames - split),
+            (jnp.logical_and(me >= span, me < last), frames),
+        ):
+            @pl.when(chosen)
+            def _():
+                sent(count * span - kept, out_send)
+    else:
+        @pl.when(owner)
+        def _():
+            sent_rows(heads - 1)
+            sent(frames * span - kept, out_send)
+
+        @pl.when(jnp.logical_not(owner))
+        def _():
+            sent_rows(heads)
 
     pltpu.make_async_copy(out_ref, out_ref, out_recv).wait()
 
@@ -368,12 +436,13 @@
             pltpu.SemaphoreType.DMA((3,)),
             pltpu.SemaphoreType.DMA((1,)),
             pltpu.SemaphoreType.DMA,
-            pltpu.SemaphoreType.DMA((heads,)),
+            pltpu.SemaphoreType.DMA,
             pltpu.SemaphoreType.DMA((frames,)),
-            pltpu.SemaphoreType.DMA((heads,)),
+            pltpu.SemaphoreType.DMA,
             pltpu.SemaphoreType.DMA((frames,)),
-            pltpu.SemaphoreType.DMA((devices,)),
             pltpu.SemaphoreType.DMA,
+            pltpu.SemaphoreType.DMA,
+            pltpu.SemaphoreType.REGULAR,
         ],
         compiler_params=pltpu.CompilerParams(has_side_effects=True, collective_id=0),
         name="denoise",

time: 20.5 us -> 19.9 us (0.971)
  Pallas kernels: 19 us -> 18.4 us
    pallas_call x1, Pallas kernels: 19 us -> 18.4 us  [body(): pl.pallas_call(functools.partial(kernel, devices, segments, heads, frames...]
where the time goes in v3:
time: 19.9 us; the launch traced here: 19.7 us
  Pallas kernels  18.4 us (92%)
  local copies, waits for them, and re-layouts  0.68 us (3%)
  between operations  0.66 us (3%)
    pallas_call x1, Pallas kernels, body(): pl.pallas_call(functools.partial(kernel, devices, segments, heads, frames...  18.4 us
    unnamed x1, local copies, waits for them, and re-layouts  0.68 us

profile of v3, /device:TPU:0, one launch (start us, length us, event | category | flops | bytes accessed | tf_op | source)
XLA Modules:
  0.0 19.7 jit_solution(7383969865243151854)
XLA Ops:
  0.7 18.4 %denoise.1 = bf16[1,32,3072]{2,1,0:T(8,128)(2,1)S(1)} custom-call(s32[4]{0:T(128)} %level_hbm.1, s32[4,4]{1,0:T(4,128)} %mask_hbm.1, s32[1]{0:T(128)S(6)} %copy.8.offset_hbm, bf16[1,32,3072]{2,1,0:T(8,128)(2,1)} %state_ref.1, f32[1,7,32,3072]{3,2,1,0:T(8,128)} %bitcast.1), custom_call_target="tpu_custom_call" | custom-call | tf_op jit(solution)/shard_map/denoise/pallas_call | solution.py:418
  19.0 0.7 %copy.7 = bf16[1,32,3072]{2,1,0:T(8,128)(2,1)} copy(bf16[1,32,3072]{2,1,0:T(8,128)(2,1)S(1)} %denoise.1) | data formatting | bytes 393216

commit v4 on v3

--- a/solution.py
+++ b/solution.py
@@ -11,18 +11,23 @@
 HEAD = 128
 FRAME_TOK = 256
 
+LEAD = 2
+
 epsilon = 1e-06
 negative = -1e30
 score_scale = math.log2(math.e) / math.sqrt(HEAD)
 
 
-def owner_rounds(heads, span):
-    if heads % span or span % 2:
-        return [(0, 1, heads)]
+def owner_plan(heads, devices, span):
     groups = heads // span
-    evens = [(group * span, 2, span // 2) for group in [*range(1, groups), 0]]
-    return evens + [(first + 1, 2, count) for first, _, count in reversed(evens)]
-
+    if heads % span or span % 4 or (groups + 1) * span != devices or groups < 2:
+        return [(0, 1, heads)], [], []
+    last = devices - span
+    pairs = span // 2
+    order = [*range(1, groups), 0]
+    evens = [(group * span, 2, pairs) for group in order]
+    odds = [(group * span + 1, 2, pairs) for group in reversed(order)]
+    return evens + odds, [], [(groups - 1, last, 2, pairs), (groups, last + 1, 2, pairs)]
 
 def kernel(
     devices,
@@ -63,42 +68,51 @@
     segment = lax.axis_index("segment")
     span = FRAME_TOK // rows
     width = heads * HEAD
-    plan = owner_rounds(heads, span)
-    shared = heads % span == 0 and heads // span + 1 == frames
+    early_plan, late_plan, doubles = owner_plan(heads, devices, span)
+    shared = bool(doubles)
     last = devices - span
     my_frame = lax.div(me, span)
     my_part = lax.rem(me, span)
     my_row = pl.multiple_of(my_part * rows, rows)
 
-    owner, my_head, base = me < 0, 0, 0
-    rounds = []
-    for first, stride, count in plan:
-        rounds.append((base, first, stride, count))
+    def among(first, stride, count):
         place = me - first
         inside = jnp.logical_and(place >= 0, place < stride * count)
         if stride > 1:
             inside = jnp.logical_and(inside, lax.rem(place + stride * devices, stride) == 0)
+        return inside, lax.div(place, stride)
+
+    split = frames - 1
+    owner, my_head, base, low, high = me < 0, 0, 0, 0, frames
+    rounds, late_rounds = [], []
+    for index, (first, stride, count) in enumerate(early_plan + late_plan):
+        entry = (base, first, stride, count)
+        (rounds if index < len(early_plan) else late_rounds).append(entry)
+        inside, rank = among(first, stride, count)
         owner = jnp.logical_or(owner, inside)
-        my_head = jnp.where(inside, base + lax.div(place, stride), my_head)
-        if base == 0:
+        my_head = jnp.where(inside, base + rank, my_head)
+        if index == 0:
             early = inside
         base += count
-
-    leader = owner
-    late = me >= last
-    split = frames - 1
-    low, high = 0, frames
+    leader, late = owner, me < 0
+    lower, upper = me < 0, me < 0
+    for index, first, stride, count in doubles:
+        base, lower_first, lower_stride, _ = rounds[index]
+        late_rounds.append((base, first, stride, count))
+        inside, rank = among(first, stride, count)
+        owner = jnp.logical_or(owner, inside)
+        my_head = jnp.where(inside, base + rank, my_head)
+        upper = jnp.logical_or(upper, inside)
+        lower = jnp.logical_or(lower, among(lower_first, lower_stride, count)[0])
     if shared:
-        for base, first, stride, count in list(rounds):
-            if first < span:
-                rounds.append((base, first + last, stride, count))
-                place = me - last - first
-                inside = jnp.logical_and(place >= 0, lax.rem(place + stride * devices, stride) == 0)
-                my_head = jnp.where(inside, base + lax.div(place, stride), my_head)
-        owner = jnp.logical_or(owner, late)
-        low = jnp.where(late, split, 0)
-        high = jnp.where(me < span, split, frames)
-
+        late = me >= last
+        leader = jnp.logical_not(late)
+        low = jnp.where(upper, split, 0)
+        high = jnp.where(lower, split, frames)
+    copies = sum(entry[3] for entry in rounds + late_rounds)
+
+    second_half = 2 * me >= devices
+    far = my_part >= span - span // 4
     nxt = lax.rem(segment + 1, segments)
     barrier = pltpu.get_barrier_semaphore()
 
@@ -138,7 +152,7 @@
             lax.fori_loop(last, devices - 1, greet_reader, 0)
 
     if segments > 1:
-        for _, first, stride, count in rounds:
+        for _, first, stride, count in rounds + late_rounds:
 
             def greet_writer(index, carry):
                 greet(first + stride * index, lax.rem(segment + segments - 1, segments))
@@ -174,7 +188,7 @@
         jnp.where(diagonal, factor, 0.0), axis=0, keepdims=True
     )
 
-    greetings = heads - jnp.where(leader, 1, 0)
+    greetings = (last if shared else heads) - jnp.where(leader, 1, 0)
     if shared:
         greetings += jnp.where(late, span - 1, 0)
     if segments > 1:
@@ -219,7 +233,7 @@
 
             lax.fori_loop(0, count, each, 0)
 
-    for_heads(rounds[: len(plan)], lambda copy: copy.start())
+    for_heads(rounds, lambda copy: copy.start())
 
     if shared:
         def admit(peer, carry):
@@ -239,7 +253,7 @@
         def _():
             pl.semaphore_wait(late_sem, span)
 
-        for_heads(rounds[len(plan) :], lambda copy: copy.start())
+        for_heads(late_rounds, lambda copy: copy.start())
 
     @pl.when(owner)
     def _():
@@ -272,17 +286,24 @@
             pltpu.make_async_copy(source, goal, out_recv).start()
 
     def send_all():
-        def each(index, carry):
-            part = index
-
-            def one(turn, carry):
-                place = jnp.where(2 * me >= devices, low + turn, high - 1 - turn)
-                send_part(place, part)
-                return carry
-
-            return lax.fori_loop(0, high - low, one, carry)
-
-        lax.fori_loop(0, span, each, 0)
+        whole = jnp.logical_not(jnp.logical_or(lower, upper))
+        paths = [
+            (jnp.logical_and(whole, second_half), range(frames)),
+            (jnp.logical_and(whole, jnp.logical_not(second_half)), range(frames)[::-1]),
+        ]
+        if shared:
+            paths += [(lower, range(split)[::-1]), (upper, range(split, frames))]
+        for chosen, places in paths:
+            @pl.when(chosen)
+            def _():
+                def each(part, carry, skip):
+                    for place in places:
+                        if place >= skip:
+                            send_part(place, part)
+                    return carry
+
+                lax.fori_loop(0, LEAD, lambda part, carry: each(part, carry, 1), 0)
+                lax.fori_loop(LEAD, span, lambda part, carry: each(part, carry, 0), 0)
 
 
     def sent(count, send_sem):
@@ -322,14 +343,18 @@
             queries.append((wide * query_scale + query_shift).astype(jnp.bfloat16))
         return jnp.concatenate(queries, axis=0)
 
-    def attend(frame, queries):
+    def score(queries, other):
+        return lax.dot_general(
+            queries,
+            keys[tokens_of(other), :],
+            (((1,), (1,)), ((), ())),
+            preferred_element_type=jnp.float32,
+        )
+
+    def attend(frame, queries, part, ready=()):
+        queries = queries[part]
         scores = [
-            lax.dot_general(
-                queries,
-                keys[tokens_of(other), :],
-                (((1,), (1,)), ((), ())),
-                preferred_element_type=jnp.float32,
-            )
+            ready[other][part] if other in ready else score(queries, other)
             for other in range(frame + 1)
         ]
         top = jnp.max(scores[frame], axis=-1, keepdims=True)
@@ -347,61 +372,117 @@
                 weights, values[tokens_of(other), :], preferred_element_type=jnp.float32
             )
         attention = (summed / total).astype(jnp.bfloat16)
-        done[frame] = (
-            gathered[frame].astype(jnp.float32)
+        done[frame, part, :] = (
+            gathered[frame, part, :].astype(jnp.float32)
             + mod_row(frame, 6) * attention.astype(jnp.float32)
         ).astype(jnp.bfloat16)
 
-    def in_order(batches):
-        for batch in batches:
-            for frame in batch:
-                pltpu.make_async_copy(
-                    gathered.at[frame], gathered.at[frame], state_recv.at[frame]
-                ).wait()
-                arrived = scales.at[pl.ds(frame * span, span)]
-                pltpu.make_async_copy(arrived, arrived, scale_recv.at[frame]).wait()
-            held = [project(frame) for frame in batch]
-            for frame, queries in zip(batch, held):
-                attend(frame, queries)
+    def source_of(place):
+        return lax.rem(place + jnp.where(segment == segments - 1, offset_ref[0], 0), frames)
+
+    lead = slice(0, LEAD * rows)
+    trail = slice(LEAD * rows, FRAME_TOK)
+    both = slice(0, FRAME_TOK)
+
+    def send_lead():
+        outgoing[0, lead, :] = done[source_of(0), lead, :]
+
+        @pl.when(low == 0)
+        def _():
+            for part in range(LEAD):
+                send_part(0, part)
+
+    def send_rest():
+        outgoing[0, trail, :] = done[source_of(0), trail, :]
+        for place in range(1, frames):
+            outgoing[place] = done[source_of(place)]
+        send_all()
+
+    def await_rows(frame):
+        pltpu.make_async_copy(
+            gathered.at[frame], gathered.at[frame], state_recv.at[frame]
+        ).wait()
+        arrived = scales.at[pl.ds(frame * span, span)]
+        pltpu.make_async_copy(arrived, arrived, scale_recv.at[frame]).wait()
+
+    def at_once():
+        for frame in range(frames):
+            await_rows(frame)
+        held = [project(frame) for frame in range(frames)]
+        for frame in range(frames):
+            attend(frame, held[frame], both)
+        send_lead()
+
+    def last_apart(apart):
+        for frame in range(frames - 1):
+            await_rows(frame)
+        held = [project(frame) for frame in range(frames - 1)]
+        for frame in range(frames - 1):
+            attend(frame, held[frame], both)
+        await_rows(frames - 1)
+        queries = project(frames - 1)
+        attend(frames - 1, queries, lead if apart else both)
+        send_lead()
+        if apart:
+            attend(frames - 1, queries, trail)
+
+    def as_they_come(apart):
+        for frame in range(frames - 2):
+            await_rows(frame)
+            attend(frame, project(frame), both)
+        final = frames - 1
+        await_rows(final)
+        queries = project(final)
+        ready = {
+            other: score(queries, other) for other in range(frames) if other != final - 1
+        }
+        await_rows(final - 1)
+        others = project(final - 1)
+        first = lead if apart else both
+        attend(final - 1, others, first)
+        attend(final, queries, first, ready)
+        send_lead()
+        if apart:
+            attend(final - 1, others, trail)
+            attend(final, queries, trail, ready)
 
     @pl.when(owner)
     def _():
         mod_copy.wait()
         for copy in scalar_copies:
             copy.wait()
-        @pl.when(jnp.logical_or(2 * me >= devices, early))
-        def _():
-            in_order([list(range(frames))])
-
-        @pl.when(jnp.logical_not(jnp.logical_or(2 * me >= devices, early)))
-        def _():
-            in_order([[f] for f in range(frames - 2)] + [[frames - 2, frames - 1]])
-
-        shift = jnp.where(segment == segments - 1, offset_ref[0], 0)
-        for place in range(frames):
-            outgoing[place] = done[lax.rem(place + shift, frames)]
-        send_all()
-
-    kept = 1 if segments == 1 else 0
-    if shared:
-        sent_rows(heads + span - 1)
-        for chosen, count in (
-            (me < span, split),
-            (late, frames - split),
-            (jnp.logical_and(me >= span, me < last), frames),
+        middle = jnp.logical_and(second_half, jnp.logical_not(late))
+        at_start = jnp.logical_or(early, late)
+        rest = jnp.logical_not(jnp.logical_or(second_half, early))
+        for chosen, run in (
+            (at_start, at_once),
+            (jnp.logical_and(middle, far), lambda: last_apart(True)),
+            (jnp.logical_and(middle, jnp.logical_not(far)), lambda: last_apart(False)),
+            (jnp.logical_and(rest, far), lambda: as_they_come(True)),
+            (jnp.logical_and(rest, jnp.logical_not(far)), lambda: as_they_come(False)),
         ):
             @pl.when(chosen)
             def _():
+                run()
+
+        send_rest()
+
+    kept = 1 if segments == 1 else 0
+
+    @pl.when(owner)
+    def _():
+        sent_rows(copies - 1)
+
+    @pl.when(jnp.logical_not(owner))
+    def _():
+        sent_rows(copies)
+
+    whole = jnp.logical_and(owner, jnp.logical_not(jnp.logical_or(lower, upper)))
+    for chosen, count in ((whole, frames), (lower, split), (upper, frames - split)):
+        if shared or count == frames:
+            @pl.when(chosen)
+            def _():
                 sent(count * span - kept, out_send)
-    else:
-        @pl.when(owner)
-        def _():
-            sent_rows(heads - 1)
-            sent(frames * span - kept, out_send)
-
-        @pl.when(jnp.logical_not(owner))
-        def _():
-            sent_rows(heads)
 
     pltpu.make_async_copy(out_ref, out_ref, out_recv).wait()
 

time: 19.9 us -> 19.3 us (0.970)
  Pallas kernels: 18.4 us -> 17.8 us
    pallas_call x1, Pallas kernels: 18.4 us -> 17.8 us  [body(): pl.pallas_call(functools.partial(kernel, devices, segments, heads, frames...]
where the time goes in v4:
time: 19.3 us; the launch traced here: 19.1 us
  Pallas kernels  17.8 us (92%)
  local copies, waits for them, and re-layouts  0.68 us (4%)
  between operations  0.66 us (3%)
    pallas_call x1, Pallas kernels, body(): pl.pallas_call(functools.partial(kernel, devices, segments, heads, frames...  17.8 us
    unnamed x1, local copies, waits for them, and re-layouts  0.68 us

profile of v4, /device:TPU:0, one launch (start us, length us, event | category | flops | bytes accessed | tf_op | source)
XLA Modules:
  0.0 19.1 jit_solution(2337939593515205232)
XLA Ops:
  0.7 17.8 %denoise.1 = bf16[1,32,3072]{2,1,0:T(8,128)(2,1)S(1)} custom-call(s32[4]{0:T(128)} %level_hbm.1, s32[4,4]{1,0:T(4,128)} %mask_hbm.1, s32[1]{0:T(128)S(6)} %copy.8.offset_hbm, bf16[1,32,3072]{2,1,0:T(8,128)(2,1)} %state_ref.1, f32[1,7,32,3072]{3,2,1,0:T(8,128)} %bitcast.1), custom_call_target="tpu_custom_call" | custom-call | tf_op jit(solution)/shard_map/denoise/pallas_call | solution.py:499
  18.5 0.7 %copy.7 = bf16[1,32,3072]{2,1,0:T(8,128)(2,1)} copy(bf16[1,32,3072]{2,1,0:T(8,128)(2,1)S(1)} %denoise.1) | data formatting | bytes 393216

commit v5 on v4

--- a/solution.py
+++ b/solution.py
@@ -59,7 +59,6 @@
     state_send,
     state_recv,
     scale_send,
-    scale_recv,
     out_send,
     out_recv,
     late_sem,
@@ -209,7 +208,7 @@
                 src_ref=scale_out,
                 dst_ref=scales.at[me],
                 send_sem=scale_send,
-                recv_sem=scale_recv.at[my_frame],
+                recv_sem=state_recv.at[my_frame],
                 device_id={"frame": peer},
                 device_id_type=pl.DeviceIdType.MESH,
             ),
@@ -262,7 +261,7 @@
             gathered.at[my_frame, pl.ds(my_row, rows), :],
             state_recv.at[my_frame],
         ).start()
-        pltpu.make_async_copy(scale_out, scales.at[me], scale_recv.at[my_frame]).start()
+        pltpu.make_async_copy(scale_out, scales.at[me], state_recv.at[my_frame]).start()
 
     def send_part(place, part):
         target = place * span + part
@@ -399,19 +398,19 @@
         send_all()
 
     def await_rows(frame):
-        pltpu.make_async_copy(
-            gathered.at[frame], gathered.at[frame], state_recv.at[frame]
-        ).wait()
-        arrived = scales.at[pl.ds(frame * span, span)]
-        pltpu.make_async_copy(arrived, arrived, scale_recv.at[frame]).wait()
-
-    def at_once():
+        arrived = keys.at[pl.ds(0, span * (rows + 2)), :]
+        pltpu.make_async_copy(arrived, arrived, state_recv.at[frame]).wait()
+
+    def at_once(apart):
         for frame in range(frames):
             await_rows(frame)
         held = [project(frame) for frame in range(frames)]
         for frame in range(frames):
-            attend(frame, held[frame], both)
+            attend(frame, held[frame], lead if apart else both)
         send_lead()
+        if apart:
+            for frame in range(frames):
+                attend(frame, held[frame], trail)
 
     def last_apart(apart):
         for frame in range(frames - 1):
@@ -451,19 +450,22 @@
         mod_copy.wait()
         for copy in scalar_copies:
             copy.wait()
+        even = lax.rem(me, 2) == 0
         middle = jnp.logical_and(second_half, jnp.logical_not(late))
-        at_start = jnp.logical_or(early, late)
         rest = jnp.logical_not(jnp.logical_or(second_half, early))
-        for chosen, run in (
-            (at_start, at_once),
-            (jnp.logical_and(middle, far), lambda: last_apart(True)),
-            (jnp.logical_and(middle, jnp.logical_not(far)), lambda: last_apart(False)),
-            (jnp.logical_and(rest, far), lambda: as_they_come(True)),
-            (jnp.logical_and(rest, jnp.logical_not(far)), lambda: as_they_come(False)),
+        for chosen, run, apart in (
+            (jnp.logical_or(early, late), at_once, False),
+            (jnp.logical_and(middle, even), at_once, None),
+            (jnp.logical_and(middle, jnp.logical_not(even)), last_apart, None),
+            (rest, as_they_come, None),
         ):
-            @pl.when(chosen)
-            def _():
-                run()
+            for split_rows in (False, True) if apart is None else (apart,):
+                ways = far if split_rows else jnp.logical_not(far)
+                here = chosen if apart is not None else jnp.logical_and(chosen, ways)
+
+                @pl.when(here)
+                def _():
+                    run(split_rows)
 
         send_rest()
 
@@ -520,7 +522,6 @@
             pltpu.SemaphoreType.DMA,
             pltpu.SemaphoreType.DMA((frames,)),
             pltpu.SemaphoreType.DMA,
-            pltpu.SemaphoreType.DMA((frames,)),
             pltpu.SemaphoreType.DMA,
             pltpu.SemaphoreType.DMA,
             pltpu.SemaphoreType.REGULAR,

time: 19.3 us -> 19.2 us (level)
  no operation moved by 1% of the time
where the time goes in v5:
time: 19.2 us; the launch traced here: 19.1 us
  Pallas kernels  17.7 us (92%)
  local copies, waits for them, and re-layouts  0.68 us (4%)
  between operations  0.66 us (3%)
    pallas_call x1, Pallas kernels, body(): pl.pallas_call(functools.partial(kernel, devices, segments, heads, frames...  17.7 us
    unnamed x1, local copies, waits for them, and re-layouts  0.68 us

profile of v5, /device:TPU:0, one launch (start us, length us, event | category | flops | bytes accessed | tf_op | source)
XLA Modules:
  0.0 19.1 jit_solution(10597755750463186330)
XLA Ops:
  0.7 17.7 %denoise.1 = bf16[1,32,3072]{2,1,0:T(8,128)(2,1)S(1)} custom-call(s32[4]{0:T(128)} %level_hbm.1, s32[4,4]{1,0:T(4,128)} %mask_hbm.1, s32[1]{0:T(128)S(6)} %copy.8.offset_hbm, bf16[1,32,3072]{2,1,0:T(8,128)(2,1)} %state_ref.1, f32[1,7,32,3072]{3,2,1,0:T(8,128)} %bitcast.1), custom_call_target="tpu_custom_call" | custom-call | tf_op jit(solution)/shard_map/denoise/pallas_call | solution.py:501
  18.4 0.7 %copy.7 = bf16[1,32,3072]{2,1,0:T(8,128)(2,1)} copy(bf16[1,32,3072]{2,1,0:T(8,128)(2,1)S(1)} %denoise.1) | data formatting | bytes 393216
